TPU v7x, 128 devices: a whole 4x4x4 slice. The times are simulated.
128 devices in a mesh: gx: 8 (over x, core), gy: 16 (over y, z).
Axes of the slice: x: 4, y: 4, z: 4, core: 2. Of those that a mesh axis runs over, the one named last changes fastest.
Arguments:
- tokens: bfloat16 [512, 8192], P('gy', 'gx'), may hold values from -6 to 6
- up_old: bfloat16 [32768, 8192], P(('gx', 'gy')), may hold values from -0.0625 to 0.0625
- down_old: bfloat16 [32768, 8192], P(('gx', 'gy')), may hold values from -0.0625 to 0.0625
- old_slot: int32 [256], replicated, may hold values from 0 to 255, as said below
- new_owner: int32 [256], replicated, may hold values from 0 to 127, as said below
- hot_rank: int32 [256], replicated, may hold values from 0 to 1, as said below
- route: int32 [512], replicated, may hold values from 0 to 511, each once
Outputs:
- up_new: bfloat16 [32768, 8192], P(('gx', 'gy'))
- down_new: bfloat16 [32768, 8192], P(('gx', 'gy'))
- mixed: bfloat16 [512, 8192], P('gy', 'gx')
Inputs may be any that keep to these rules, and one draw needn't show every extreme that they name: `old_slot`: each slot number appears exactly once. `new_owner`: each device index is the new owner of exactly 2 blocks. `hot_rank`: the blocks of one new owner have distinct ranks.
All inputs are finite; a program needn't handle non-finite values.
Results may differ from a plain program's by a relative error of at most 0.0049.
Values may be sent and summed in bfloat16 or wider, within the bound.
A program may use at most 128 MiB of HBM per device.

v0:
```python
import jax
import jax.numpy as jnp
from jax import lax
from jax.sharding import PartitionSpec as P

BLOCK = 128


def split_up(shard, dim, peers):
    lengths = shard.shape
    parts = shard.reshape(*lengths[:dim], peers, lengths[dim] // peers, *lengths[dim + 1 :])
    return jnp.moveaxis(parts, dim, 0)


def laid_out(parts, dim):
    parts = jnp.moveaxis(parts, 0, dim)
    lengths = parts.shape
    return parts.reshape(*lengths[:dim], lengths[dim] * lengths[dim + 1], *lengths[dim + 2 :])


def exchange_both(shard, axis, axes, splits, concats):
    sizes = [lax.axis_size(a) for a in axes]
    parts = split_up(shard, splits[0], sizes[0])
    parts = jnp.moveaxis(split_up(parts, splits[1] + 1, sizes[1]), 0, 1)
    inside = parts.shape[2:]
    parts = parts.reshape(-1, *inside)
    parts = lax.all_to_all(parts, axis, split_axis=0, concat_axis=0, tiled=True)
    parts = laid_out(parts.reshape(*sizes, *inside), concats[0] + 1)
    return laid_out(parts, concats[1])


def sum_at_owner(shard, axis, dim):
    parts = split_up(shard, dim, lax.axis_size(axis))
    arrived = lax.all_to_all(parts, axis, split_axis=0, concat_axis=0, tiled=True)
    return arrived.sum(axis=0)


def layer_terms(ordered, up_rows, down_rows):
    pre = lax.dot_general(
        ordered, up_rows, (((1,), (1,)), ((), ())), preferred_element_type=jnp.float32
    )
    hidden = jax.nn.gelu(pre, approximate=False).astype(jnp.bfloat16)
    return jnp.dot(hidden, down_rows, preferred_element_type=jnp.float32)


def relocate(up_old, down_old, old_slot, new_owner, hot_rank):
    held = up_old.shape[0] // BLOCK
    width = up_old.shape[1]
    shaped = (up_old.reshape(held, BLOCK, width), down_old.reshape(held, BLOCK, width))
    across_x = lax.axis_size("gx")
    across_y = lax.axis_size("gy")
    sectioned = (
        exchange_both(shaped[0], ("gx", "gy"), ("gx", "gy"), (1, 1), (0, 0)),
        exchange_both(shaped[1], ("gx", "gy"), ("gx", "gy"), (1, 1), (0, 0)),
    )
    share = sectioned[0].shape[1]

    def reorder(arr):
        arr = arr.reshape(across_y, across_x, held, share, width)
        return jnp.transpose(arr, (1, 0, 2, 3, 4)).reshape(across_x * across_y * held, share, width)

    spread = (reorder(sectioned[0]), reorder(sectioned[1]))
    total = spread[0].shape[0]
    new_slot = new_owner * held + hot_rank
    source = jnp.zeros((total,), jnp.int32).at[new_slot].set(old_slot)
    picked = (jnp.take(spread[0], source, axis=0), jnp.take(spread[1], source, axis=0))
    landed = (
        lax.all_to_all(picked[0], ("gx", "gy"), split_axis=0, concat_axis=1, tiled=True),
        lax.all_to_all(picked[1], ("gx", "gy"), split_axis=0, concat_axis=1, tiled=True),
    )
    return (landed[0].reshape(held * BLOCK, width), landed[1].reshape(held * BLOCK, width))


def shards(tokens, up_old, down_old, old_slot, new_owner, hot_rank, route):
    feature_rows = lax.all_gather(tokens, "gx", axis=1, tiled=True)
    everyone = lax.all_gather(feature_rows, "gy", axis=0, tiled=True)
    ordered = jnp.take(everyone, route, axis=0)
    up_new, down_new = relocate(up_old, down_old, old_slot, new_owner, hot_rank)
    partial_out = layer_terms(ordered, up_new, down_new)
    by_columns = lax.psum_scatter(partial_out, "gx", scatter_dimension=1, tiled=True)
    summed = sum_at_owner(by_columns, "gy", 0)
    return (up_new, down_new, summed.astype(jnp.bfloat16))


def solution(mesh):
    in_specs = (P("gy", "gx"), P(("gx", "gy"), None), P(("gx", "gy"), None), P(), P(), P(), P())
    out_specs = (P(("gx", "gy"), None), P(("gx", "gy"), None), P("gy", "gx"))
    return jax.shard_map(shards, mesh=mesh, in_specs=in_specs, out_specs=out_specs, check_vma=False)
```

profile of v0, /device:TPU:0, one launch (start us, length us, event | category | flops | bytes accessed | tf_op | source)
XLA Modules:
  0.0 561.5 jit_solution(2574933312884499092)
XLA Ops:
  7.2 8.6 %copy.24 = bf16[2,8,16,8192]{3,0,2,1:T(2,128)(2,1)} copy(bf16[2,8,16,8192]{3,2,1,0:T(8,128)(2,1)} %bitcast.36) | data formatting | bytes 8388608 | tf_op jit(solution)/shard_map/reshape;reshape | solution.py:11
  15.7 0.0 copy-start
  15.7 11.7 %all-to-all-start = ((bf16[128,2,1,8192]{3,1,2,0:T(2,128)(2,1)}), bf16[128,2,1,8192]{3,1,2,0:T(2,128)(2,1)}, u32[]{:S(2)}, u32[]{:S(2)}) async-start(bf16[128,2,1,8192]{3,1,2,0:T(2,128)(2,1)} %bitcast.33), calls=%async_computation | async-start | bytes 8388608 | tf_op jit(solution)/shard_map/all_to_all | solution.py:27
  27.5 0.0 all-gather.2.cloned.1.call-start
  27.5 0.0 copy-done
  27.5 55.9 %all_gather.6 = bf16[32,8192]{1,0:T(8,128)(2,1)} all-gather(bf16[32,1024]{1,0:T(8,128)(2,1)S(1)} %copy-done), channel_id=1, replica_groups=mesh['gx'=8,'gy'=16] {'gx'}, dimensions={1}, use_global_device_ids=true | all-gather | bytes 589824 | tf_op jit(solution)/shard_map/all_gather | solution.py:75
  83.5 0.0 all-gather.2.cloned.1.call-update
  83.5 8.6 %copy.27 = bf16[2,8,16,8192]{3,0,2,1:T(2,128)(2,1)} copy(bf16[2,8,16,8192]{3,2,1,0:T(8,128)(2,1)} %bitcast.37) | data formatting | bytes 8388608 | tf_op jit(solution)/shard_map/reshape;reshape | solution.py:11
  92.1 0.0 all-to-all-done
  92.1 0.0 copy-start.2
  92.1 0.0 copy-start.3
  92.1 10.7 %all-to-all-start.2 = ((bf16[128,2,1,8192]{3,1,2,0:T(2,128)(2,1)}), bf16[128,2,1,8192]{3,1,2,0:T(2,128)(2,1)}, u32[]{:S(2)}, u32[]{:S(2)}) async-start(bf16[128,2,1,8192]{3,1,2,0:T(2,128)(2,1)} %bitcast.32), calls=%async_computation.2 | async-start | bytes 8388608 | tf_op jit(solution)/shard_map/all_to_all | solution.py:27
  102.8 0.0 copy-done.2
  102.8 0.0 copy-done.3
  102.8 1.6 scatter_custom_fusion
  104.4 7.2 %reshape.111 = bf16[256,8192]{1,0:T(8,128)(2,1)} reshape(bf16[128,2,1,8192]{3,1,2,0:T(2,128)(2,1)} %all-to-all-done) | data formatting | bytes 8388608 | tf_op jit(solution)/shard_map/jit(_take)/Arg_0.7 | solution.py:66
  111.6 11.7 %gather_fusion.1 = bf16[256,8192]{1,0:T(8,128)(2,1)} fusion(bf16[256,8192]{1,0:T(8,128)(2,1)} %reshape.111, s32[1024]{0:T(1024)S(1)} %pad_clamp_fusion.1), kind=kCustom, calls=%fused_computation.clone | custom fusion | bytes 8389632 | tf_op jit(solution)/shard_map/jit(_take)/gather | solution.py:66
  123.3 32.9 %all-to-all-done.2 = bf16[128,2,1,8192]{3,1,2,0:T(2,128)(2,1)} async-done(((bf16[128,2,1,8192]{3,1,2,0:T(2,128)(2,1)}), bf16[128,2,1,8192]{3,1,2,0:T(2,128)(2,1)}, u32[]{:S(2)}, u32[]{:S(2)}) %all-to-all-start.2) | async-done | bytes 4194336 | tf_op jit(solution)/shard_map/all_to_all | solution.py:27
  156.3 7.7 %reshape.115 = bf16[256,8192]{1,0:T(8,128)(2,1)} reshape(bf16[128,2,1,8192]{3,1,2,0:T(2,128)(2,1)} %all-to-all-done.2) | data formatting | bytes 8388608 | tf_op jit(solution)/shard_map/jit(_take)/Arg_0.7 | solution.py:66
  164.0 11.7 %gather_fusion.2 = bf16[256,8192]{1,0:T(8,128)(2,1)} fusion(bf16[256,8192]{1,0:T(8,128)(2,1)} %reshape.115, s32[1024]{0:T(1024)S(1)} %pad_clamp_fusion.1), kind=kCustom, calls=%fused_computation.1.clone | custom fusion | bytes 8389632 | tf_op jit(solution)/shard_map/jit(_take)/gather | solution.py:66
  175.7 6.0 %bitcast_select_fusion = (bf16[256,1,8192]{2,0,1:T(8,128)(2,1)}, bf16[256,1,8192]{2,0,1:T(8,128)(2,1)}) fusion(bf16[256,8192]{1,0:T(8,128)(2,1)} %gather_fusion.2, pred[256]{0:T(512)(128)(4,1)S(1)} %compare_and_fusion, bf16[256,8192]{1,0:T(8,128)(2,1)} %gather_fusion.1), kind=kLoop, calls=%fused_computation.7 | loop fusion | flops 4194304 | bytes 16777472 | tf_op jit(solution)/shard_map/jit(_take)/select_n | solution.py:66
  181.8 0.5 broadcast.59
  182.3 6.8 %reduce.2 = bf16[256,8192]{1,0:T(8,128)(2,1)} reduce(bf16[256,1,8192]{2,0,1:T(8,128)(2,1)} %get-tuple-element.5, bf16[]{:T(256)} %broadcast.59), dimensions={1}, to_apply=%copy.25.reduce_sub_computation | reduce | bytes 8388610 | tf_op jit(solution)/shard_map/jit(_take)/select_n | solution.py:66
  189.1 7.6 %reshape.125 = bf16[128,2,8192]{2,1,0:T(2,128)(2,1)} reshape(bf16[256,8192]{1,0:T(8,128)(2,1)} %reduce.2) | data formatting | bytes 8388608
  196.7 7.7 %all-to-all-start.1 = ((bf16[128,2,8192]{2,1,0:T(2,128)(2,1)}), bf16[128,2,8192]{2,1,0:T(2,128)(2,1)}, u32[]{:S(2)}, u32[]{:S(2)}) async-start(bf16[128,2,8192]{2,1,0:T(2,128)(2,1)} %reshape.125), calls=%async_computation.1 | async-start | bytes 8388608 | tf_op jit(solution)/shard_map/all_to_all | solution.py:68
  204.5 6.7 %reduce.3 = bf16[256,8192]{1,0:T(8,128)(2,1)} reduce(bf16[256,1,8192]{2,0,1:T(8,128)(2,1)} %get-tuple-element.4, bf16[]{:T(256)} %broadcast.59), dimensions={1}, to_apply=%copy.28.reduce_sub_computation | reduce | bytes 8388610 | tf_op jit(solution)/shard_map/jit(_take)/select_n | solution.py:66
  211.2 7.6 %reshape.127 = bf16[128,2,8192]{2,1,0:T(2,128)(2,1)} reshape(bf16[256,8192]{1,0:T(8,128)(2,1)} %reduce.3) | data formatting | bytes 8388608
  218.8 0.0 copy-start.1
  218.8 38.0 %all-to-all-done.1 = bf16[128,2,8192]{2,1,0:T(2,128)(2,1)} async-done(((bf16[128,2,8192]{2,1,0:T(2,128)(2,1)}), bf16[128,2,8192]{2,1,0:T(2,128)(2,1)}, u32[]{:S(2)}, u32[]{:S(2)}) %all-to-all-start.1) | async-done | bytes 4194336 | tf_op jit(solution)/shard_map/all_to_all | solution.py:68
  256.8 5.8 %all-to-all-start.3 = ((bf16[128,2,8192]{2,1,0:T(2,128)(2,1)}), bf16[128,2,8192]{2,1,0:T(2,128)(2,1)}, u32[]{:S(2)}, u32[]{:S(2)}) async-start(bf16[128,2,8192]{2,1,0:T(2,128)(2,1)} %reshape.127), calls=%async_computation.3 | async-start | bytes 8388608 | tf_op jit(solution)/shard_map/all_to_all | solution.py:69
  262.6 0.0 reduce-scatter.2.cloned.1.call-start
  262.7 0.0 copy-done.1
  262.7 19.8 %reshape.126 = bf16[256,1,8192]{2,1,0:T(2,128)(2,1)} reshape(bf16[128,2,8192]{2,1,0:T(2,128)(2,1)} %all-to-all-done.1) | data formatting | bytes 8388608
  282.5 26.3 %reduce = bf16[256,8192]{1,0:T(8,128)(2,1)} reduce(bf16[256,1,8192]{2,1,0:T(2,128)(2,1)} %reshape.126, bf16[]{:T(256)} %constant.92), dimensions={1}, to_apply=%all_to_all.32.reduce_sub_computation | reduce | bytes 8388610 | tf_op jit(solution)/shard_map/all_to_all | solution.py:68
  308.7 7.7 %all_to_all.33 = bf16[128,2,1,8192]{3,1,0,2:T(2,128)(2,1)} reshape(bf16[256,8192]{1,0:T(8,128)(2,1)} %reduce) | data formatting | bytes 8388608 | tf_op jit(solution)/shard_map/all_to_all | solution.py:68
  316.4 6.9 %copy.26 = bf16[2,128,1,8192]{3,1,0,2:T(8,128)(2,1)} copy(bf16[2,128,1,8192]{3,0,1,2:T(2,128)(2,1)} %bitcast.34) | data formatting | bytes 8388608 | tf_op jit(solution)/shard_map/all_to_all | solution.py:68
  323.3 0.0 all-to-all-done.3
  323.3 19.8 %reshape.128 = bf16[256,1,8192]{2,1,0:T(2,128)(2,1)} reshape(bf16[128,2,8192]{2,1,0:T(2,128)(2,1)} %all-to-all-done.3) | data formatting | bytes 8388608
  343.1 26.3 %reduce.1 = bf16[256,8192]{1,0:T(8,128)(2,1)} reduce(bf16[256,1,8192]{2,1,0:T(2,128)(2,1)} %reshape.128, bf16[]{:T(256)} %constant.92), dimensions={1}, to_apply=%all_to_all.36.reduce_sub_computation | reduce | bytes 8388610 | tf_op jit(solution)/shard_map/all_to_all | solution.py:69
  369.3 7.9 %all_to_all.37 = bf16[128,2,1,8192]{3,1,0,2:T(2,128)(2,1)} reshape(bf16[256,8192]{1,0:T(8,128)(2,1)} %reduce.1) | data formatting | bytes 8388608 | tf_op jit(solution)/shard_map/all_to_all | solution.py:69
  377.2 6.9 %copy.29 = bf16[2,128,1,8192]{3,1,0,2:T(8,128)(2,1)} copy(bf16[2,128,1,8192]{3,0,1,2:T(2,128)(2,1)} %bitcast.35) | data formatting | bytes 8388608 | tf_op jit(solution)/shard_map/all_to_all | solution.py:69
  384.1 0.0 all-gather.2.cloned.1.call-done
  384.1 20.2 %gather_fusion = bf16[512,8192]{1,0:T(8,128)(2,1)} fusion(bf16[512,8192]{1,0:T(8,128)(2,1)} %all-gather.2.cloned.1.call-done, s32[1024]{0:T(1024)S(1)} %pad_clamp_fusion), kind=kCustom, calls=%fused_computation.2 | custom fusion | bytes 16779264 | tf_op jit(solution)/shard_map/jit(_take)/gather | solution.py:77
  404.3 21.5 %fusion.17 = f32[512,8192]{1,0:T(8,128)} fusion(bf16[256,8192]{1,0:T(8,128)(2,1)} %bitcast.40, bf16[256,8192]{1,0:T(8,128)(2,1)} %bitcast.38, bf16[512,8192]{1,0:T(8,128)(2,1)} %gather_fusion, pred[512]{0:T(512)(128)(4,1)S(1)} %compare_and_fusion.1), kind=kOutput, calls=%fused_computation.29 | convolution fusion | flops 4307681280 | bytes 33554944 | tf_op jit(solution)/shard_map/dot_general | solution.py:43
  425.7 0.0 reduce-scatter.2.cloned.1.call-update
  425.8 92.9 %reduce-scatter.2.cloned.1.call-done = f32[512,1024]{1,0:T(8,128)} async-done(((f32[512,8192]{1,0:T(8,128)}), f32[512,1024]{1,0:T(8,128)}) %reduce-scatter.2.cloned.1.call-update) | async-done | bytes 2097168 | tf_op jit(solution)/shard_map/reduce_scatter | solution.py:80
  518.6 34.8 %all_to_all.45 = f32[16,32,1024]{2,1,0:T(8,128)S(1)} all-to-all(f32[16,32,1024]{2,1,0:T(8,128)} %bitcast.42), channel_id=1, replica_groups=mesh['gx'=8,'gy'=16] {'gy'}, dimensions={0} | all-to-all | bytes 4194304 | tf_op jit(solution)/shard_map/all_to_all | solution.py:34
  553.5 0.7 reduce_sum.9
  (7 shorter events, 0.0 us)
Async XLA Ops:
  15.7 11.8 %copy-start = (bf16[32,1024]{1,0:T(8,128)(2,1)S(1)}, bf16[32,1024]{1,0:T(8,128)(2,1)}, u32[]{:S(2)}) copy-start(bf16[32,1024]{1,0:T(8,128)(2,1)} %param.9) | copy-start | bytes 196612
  15.7 76.3 %all-to-all-start = ((bf16[128,2,1,8192]{3,1,2,0:T(2,128)(2,1)}), bf16[128,2,1,8192]{3,1,2,0:T(2,128)(2,1)}, u32[]{:S(2)}, u32[]{:S(2)}) async-start(bf16[128,2,1,8192]{3,1,2,0:T(2,128)(2,1)} %bitcast.33), calls=%async_computation | async-start | bytes 8388608 | tf_op jit(solution)/shard_map/all_to_all | solution.py:27
  27.5 356.7 %all-gather.2.cloned.1.call-start = ((), (), s32[]{:S(2)}) async-start(), calls=%async_computation.6 | async-start | bytes 8912896 | tf_op jit(solution)/shard_map/all_gather | solution.py:76
  92.1 10.8 %copy-start.2 = (s32[256]{0:T(256)S(1)}, s32[256]{0:T(256)}, u32[]{:S(2)}) copy-start(s32[256]{0:T(256)} %param.14) | copy-start | bytes 3076
  92.1 10.8 %copy-start.3 = (s32[256]{0:T(256)S(1)}, s32[256]{0:T(256)}, u32[]{:S(2)}) copy-start(s32[256]{0:T(256)} %param.13) | copy-start | bytes 3076
  92.1 64.2 %all-to-all-start.2 = ((bf16[128,2,1,8192]{3,1,2,0:T(2,128)(2,1)}), bf16[128,2,1,8192]{3,1,2,0:T(2,128)(2,1)}, u32[]{:S(2)}, u32[]{:S(2)}) async-start(bf16[128,2,1,8192]{3,1,2,0:T(2,128)(2,1)} %bitcast.32), calls=%async_computation.2 | async-start | bytes 8388608 | tf_op jit(solution)/shard_map/all_to_all | solution.py:27
  196.7 60.0 %all-to-all-start.1 = ((bf16[128,2,8192]{2,1,0:T(2,128)(2,1)}), bf16[128,2,8192]{2,1,0:T(2,128)(2,1)}, u32[]{:S(2)}, u32[]{:S(2)}) async-start(bf16[128,2,8192]{2,1,0:T(2,128)(2,1)} %reshape.125), calls=%async_computation.1 | async-start | bytes 8388608 | tf_op jit(solution)/shard_map/all_to_all | solution.py:68
  218.8 43.8 %copy-start.1 = (s32[512]{0:T(512)S(1)}, s32[512]{0:T(512)}, u32[]{:S(2)}) copy-start(s32[512]{0:T(512)} %param.15) | copy-start | bytes 6148
  256.8 66.5 %all-to-all-start.3 = ((bf16[128,2,8192]{2,1,0:T(2,128)(2,1)}), bf16[128,2,8192]{2,1,0:T(2,128)(2,1)}, u32[]{:S(2)}, u32[]{:S(2)}) async-start(bf16[128,2,8192]{2,1,0:T(2,128)(2,1)} %reshape.127), calls=%async_computation.3 | async-start | bytes 8388608 | tf_op jit(solution)/shard_map/all_to_all | solution.py:69
  262.6 256.0 %reduce-scatter.2.cloned.1.call-start = ((), (), s32[]{:S(2)}) async-start(), calls=%async_computation.7 | async-start | bytes 18874368 | tf_op jit(solution)/shard_map/reduce_scatter | solution.py:80
Sparse Core Ops, SparseCore 0:
  83.6 115.8 all-gather.1
  425.9 92.7 reduce-scatter.1
where the time goes:
time: 572 us; the launch traced here: 561 us
  waiting for transfers between devices  164 us (29%)
  local copies, waits for them, and re-layouts  162 us (28%)
  blocking collectives  90.8 us (16%)
  other arithmetic  72.9 us (13%)
  starting transfers between devices  36.1 us (6%)
  matrix products  21.5 us (4%)
  between operations  14.6 us (3%)
    reduce_scatter x1, waiting for transfers between devices, shards(): lax.psum_scatter(partial_out, 'gx', scatter_dimension=1, tiled=True)  92.9 us
    all_gather x1, blocking collectives, shards(): feature_rows = lax.all_gather(tokens, 'gx', axis=1, tiled=True)  55.9 us
    unnamed x12, local copies, waits for them, and re-layouts  54.8 us
    all_to_all x1, waiting for transfers between devices, relocate(): lax.all_to_all(picked[0], ('gx', 'gy'), split_axis=0, concat_axis=1, tile...  38 us
    all_to_all x1, blocking collectives, sum_at_owner(): lax.all_to_all(parts, axis, split_axis=0, concat_axis=0, tiled=True)  34.8 us
    all_to_all x2, waiting for transfers between devices, exchange_both(): parts = lax.all_to_all(parts, axis, split_axis=0, concat_axis=0, tiled=True)  32.9 us
    all_to_all x1, other arithmetic, relocate(): lax.all_to_all(picked[0], ('gx', 'gy'), split_axis=0, concat_axis=1, tile...  26.3 us
    all_to_all x1, other arithmetic, relocate(): lax.all_to_all(picked[1], ('gx', 'gy'), split_axis=0, concat_axis=1, tile...  26.3 us
  transfers between devices with their start and end apart: 6, of which 3 were waited for; matrix products, arithmetic and copies ran while one was open for 34% of the time, Pallas kernels for 0%

commit v1 on v0

--- a/solution.py
+++ b/solution.py
@@ -4,6 +4,15 @@
 from jax.sharding import PartitionSpec as P
 
 BLOCK = 128
+
+
+def number_the_tails(content, ndim_at):
+    content = jnp.moveaxis(content, 0, ndim_at)
+    known = content.shape
+    k_now = content.reshape(
+        *known[:ndim_at], known[ndim_at] * known[ndim_at + 1], *known[ndim_at + 2 :]
+    )
+    return k_now
 
 
 def split_up(shard, dim, peers):
@@ -72,7 +81,27 @@
 
 
 def shards(tokens, up_old, down_old, old_slot, new_owner, hot_rank, route):
-    feature_rows = lax.all_gather(tokens, "gx", axis=1, tiled=True)
+    slots = lax.psum(1, "gx")
+    samples = []
+    j0 = 0
+    while j0 < slots:
+        samples.append((j0, (j0 + 1) % slots))
+        j0 = j0 + 1
+    sheets = []
+    for k, i in samples:
+        sheets.append((i, k))
+    small, wide_out = ([], [])
+    t = 0
+    while t < slots - 1:
+        if t % 2 == 0:
+            small.append(lax.ppermute(small[-1] if small else tokens, "gx", samples))
+        else:
+            wide_out.append(lax.ppermute(wide_out[-1] if wide_out else tokens, "gx", sheets))
+        t = t + 1
+    mat_out = jnp.stack([*small[::-1], tokens, *wide_out])
+    s_next = lax.axis_index("gx") - len(small)
+    mat_out = mat_out[(jnp.arange(slots) - s_next) % slots]
+    feature_rows = number_the_tails(mat_out, 1)
     everyone = lax.all_gather(feature_rows, "gy", axis=0, tiled=True)
     ordered = jnp.take(everyone, route, axis=0)
     up_new, down_new = relocate(up_old, down_old, old_slot, new_owner, hot_rank)

time: 572 us -> 580 us (1.014)
  blocking collectives: 90.8 us -> 34.8 us
  waiting for transfers between devices: 164 us -> 217 us
  starting transfers between devices: 36.1 us -> 45.1 us
    all_gather x1 -> x0, blocking collectives: 55.9 us -> none  [shards(): feature_rows = lax.all_gather(tokens, 'gx', axis=1, tiled=True)]
    ppermute x0 -> x7, waiting for transfers between devices: none -> 53.3 us  [the longest x4 53.3 us: shards(): small.append(lax.ppermute(small[-1] if small else tokens, 'gx', samples))]
    ppermute x0 -> x7, starting transfers between devices: none -> 8.91 us  [the longest x3 8.88 us: shards(): lax.ppermute(wide_out[-1] if wide_out else tokens, 'gx', sheets)]
    unnamed x12 -> x19, local copies, waits for them, and re-layouts: 54.8 us -> 55 us
  transfers between devices with their start and end apart: 6 -> 13, of which waited for: 3 -> 7; matrix products, arithmetic and copies ran while one was open for 34% -> 34% of each run, Pallas kernels for 0% -> 0%
where the time goes in v1:
time: 580 us; the launch traced here: 570 us
  waiting for transfers between devices  217 us (37%)
  local copies, waits for them, and re-layouts  163 us (28%)
  other arithmetic  72.9 us (13%)
  starting transfers between devices  45.1 us (8%)
  blocking collectives  34.8 us (6%)
  matrix products  21.5 us (4%)
  between operations  14.7 us (3%)
    reduce_scatter x1, waiting for transfers between devices, shards(): lax.psum_scatter(partial_out, 'gx', scatter_dimension=1, tiled=True)  92.9 us
    unnamed x19, local copies, waits for them, and re-layouts  55 us
    ppermute x4, waiting for transfers between devices, shards(): small.append(lax.ppermute(small[-1] if small else tokens, 'gx', samples))  53.3 us
    all_to_all x1, waiting for transfers between devices, relocate(): lax.all_to_all(picked[0], ('gx', 'gy'), split_axis=0, concat_axis=1, tile...  37.9 us
    all_to_all x1, blocking collectives, sum_at_owner(): lax.all_to_all(parts, axis, split_axis=0, concat_axis=0, tiled=True)  34.8 us
    all_to_all x2, waiting for transfers between devices, exchange_both(): parts = lax.all_to_all(parts, axis, split_axis=0, concat_axis=0, tiled=True)  33 us
    all_to_all x1, other arithmetic, relocate(): lax.all_to_all(picked[0], ('gx', 'gy'), split_axis=0, concat_axis=1, tile...  26.3 us
    all_to_all x1, other arithmetic, relocate(): lax.all_to_all(picked[1], ('gx', 'gy'), split_axis=0, concat_axis=1, tile...  26.3 us
  transfers between devices with their start and end apart: 13, of which 7 were waited for; matrix products, arithmetic and copies ran while one was open for 34% of the time, Pallas kernels for 0%

profile of v1, /device:TPU:0, one launch (start us, length us, event | category | flops | bytes accessed | tf_op | source)
XLA Modules:
  0.0 569.6 jit_solution(2346135480247703663)
XLA Ops:
  7.2 8.6 %copy.27 = bf16[2,8,16,8192]{3,0,2,1:T(2,128)(2,1)} copy(bf16[2,8,16,8192]{3,2,1,0:T(8,128)(2,1)} %bitcast.57) | data formatting | bytes 8388608 | tf_op jit(solution)/shard_map/reshape;reshape | solution.py:20
  15.7 0.0 copy-start
  15.7 11.7 %all-to-all-start = ((bf16[128,2,1,8192]{3,1,2,0:T(2,128)(2,1)}), bf16[128,2,1,8192]{3,1,2,0:T(2,128)(2,1)}, u32[]{:S(2)}, u32[]{:S(2)}) async-start(bf16[128,2,1,8192]{3,1,2,0:T(2,128)(2,1)} %bitcast.53), calls=%async_computation | async-start | bytes 8388608 | tf_op jit(solution)/shard_map/all_to_all | solution.py:36
  27.5 0.0 all-gather.2.cloned.1.call-start
  27.5 0.0 copy-done
  27.5 0.0 collective-permute-start
  27.5 47.5 %collective-permute-done = bf16[32,1024]{1,0:T(8,128)(2,1)S(1)} collective-permute-done((bf16[32,1024]{1,0:T(8,128)(2,1)S(1)}, bf16[32,1024]{1,0:T(8,128)(2,1)S(1)}, u32[]{:S(2)}, u32[]{:S(2)}) %collective-permute-start) | collective-permute-done | bytes 65568 | tf_op jit(solution)/shard_map/ppermute | solution.py:97
  75.0 0.0 collective-permute-start.1
  75.0 3.0 collective-permute-start.4
  78.0 1.9 collective-permute-done.1
  79.9 0.0 collective-permute-start.2
  80.0 0.0 collective-permute-done.4
  80.0 3.0 collective-permute-start.5
  82.9 1.9 collective-permute-done.2
  84.8 0.0 collective-permute-start.3
  84.9 0.0 collective-permute-done.5
  84.9 3.0 collective-permute-start.6
  87.8 1.9 collective-permute-done.3
  89.8 0.0 collective-permute-done.6
  89.9 0.6 gather_fusion
  90.4 0.9 copy.36
  91.3 0.0 all-gather.2.cloned.1.call-update
  91.3 8.6 %copy.30 = bf16[2,8,16,8192]{3,0,2,1:T(2,128)(2,1)} copy(bf16[2,8,16,8192]{3,2,1,0:T(8,128)(2,1)} %bitcast.58) | data formatting | bytes 8388608 | tf_op jit(solution)/shard_map/reshape;reshape | solution.py:20
  99.9 0.0 all-to-all-done
  99.9 0.0 copy-start.2
  99.9 0.0 copy-start.3
  99.9 10.9 %all-to-all-start.2 = ((bf16[128,2,1,8192]{3,1,2,0:T(2,128)(2,1)}), bf16[128,2,1,8192]{3,1,2,0:T(2,128)(2,1)}, u32[]{:S(2)}, u32[]{:S(2)}) async-start(bf16[128,2,1,8192]{3,1,2,0:T(2,128)(2,1)} %bitcast.54), calls=%async_computation.2 | async-start | bytes 8388608 | tf_op jit(solution)/shard_map/all_to_all | solution.py:36
  110.8 0.0 copy-done.2
  110.8 0.0 copy-done.3
  110.9 1.6 scatter_custom_fusion
  112.5 7.2 %reshape.172 = bf16[256,8192]{1,0:T(8,128)(2,1)} reshape(bf16[128,2,1,8192]{3,1,2,0:T(2,128)(2,1)} %all-to-all-done) | data formatting | bytes 8388608 | tf_op jit(solution)/shard_map/jit(_take)/Arg_0.11 | solution.py:75
  119.6 11.7 %gather_fusion.2 = bf16[256,8192]{1,0:T(8,128)(2,1)} fusion(bf16[256,8192]{1,0:T(8,128)(2,1)} %reshape.172, s32[1024]{0:T(1024)S(1)} %pad_clamp_fusion.2), kind=kCustom, calls=%fused_computation.clone | custom fusion | bytes 8389632 | tf_op jit(solution)/shard_map/jit(_take)/gather | solution.py:75
  131.3 33.0 %all-to-all-done.2 = bf16[128,2,1,8192]{3,1,2,0:T(2,128)(2,1)} async-done(((bf16[128,2,1,8192]{3,1,2,0:T(2,128)(2,1)}), bf16[128,2,1,8192]{3,1,2,0:T(2,128)(2,1)}, u32[]{:S(2)}, u32[]{:S(2)}) %all-to-all-start.2) | async-done | bytes 4194336 | tf_op jit(solution)/shard_map/all_to_all | solution.py:36
  164.4 7.7 %reshape.176 = bf16[256,8192]{1,0:T(8,128)(2,1)} reshape(bf16[128,2,1,8192]{3,1,2,0:T(2,128)(2,1)} %all-to-all-done.2) | data formatting | bytes 8388608 | tf_op jit(solution)/shard_map/jit(_take)/Arg_0.11 | solution.py:75
  172.1 11.7 %gather_fusion.3 = bf16[256,8192]{1,0:T(8,128)(2,1)} fusion(bf16[256,8192]{1,0:T(8,128)(2,1)} %reshape.176, s32[1024]{0:T(1024)S(1)} %pad_clamp_fusion.2), kind=kCustom, calls=%fused_computation.1.clone | custom fusion | bytes 8389632 | tf_op jit(solution)/shard_map/jit(_take)/gather | solution.py:75
  183.8 6.0 %bitcast_select_fusion = (bf16[256,1,8192]{2,0,1:T(8,128)(2,1)}, bf16[256,1,8192]{2,0,1:T(8,128)(2,1)}) fusion(bf16[256,8192]{1,0:T(8,128)(2,1)} %gather_fusion.3, pred[256]{0:T(512)(128)(4,1)S(1)} %compare_and_fusion, bf16[256,8192]{1,0:T(8,128)(2,1)} %gather_fusion.2), kind=kLoop, calls=%fused_computation.8 | loop fusion | flops 4194304 | bytes 16777472 | tf_op jit(solution)/shard_map/jit(_take)/select_n | solution.py:75
  189.8 0.5 broadcast.128
  190.4 6.8 %reduce.2 = bf16[256,8192]{1,0:T(8,128)(2,1)} reduce(bf16[256,1,8192]{2,0,1:T(8,128)(2,1)} %get-tuple-element.5, bf16[]{:T(256)} %broadcast.128), dimensions={1}, to_apply=%copy.28.reduce_sub_computation | reduce | bytes 8388610 | tf_op jit(solution)/shard_map/jit(_take)/select_n | solution.py:75
  197.2 7.6 %reshape.186 = bf16[128,2,8192]{2,1,0:T(2,128)(2,1)} reshape(bf16[256,8192]{1,0:T(8,128)(2,1)} %reduce.2) | data formatting | bytes 8388608
  204.8 7.7 %all-to-all-start.1 = ((bf16[128,2,8192]{2,1,0:T(2,128)(2,1)}), bf16[128,2,8192]{2,1,0:T(2,128)(2,1)}, u32[]{:S(2)}, u32[]{:S(2)}) async-start(bf16[128,2,8192]{2,1,0:T(2,128)(2,1)} %reshape.186), calls=%async_computation.1 | async-start | bytes 8388608 | tf_op jit(solution)/shard_map/all_to_all | solution.py:77
  212.5 6.7 %reduce.3 = bf16[256,8192]{1,0:T(8,128)(2,1)} reduce(bf16[256,1,8192]{2,0,1:T(8,128)(2,1)} %get-tuple-element.4, bf16[]{:T(256)} %broadcast.128), dimensions={1}, to_apply=%copy.31.reduce_sub_computation | reduce | bytes 8388610 | tf_op jit(solution)/shard_map/jit(_take)/select_n | solution.py:75
  219.2 7.7 %reshape.188 = bf16[128,2,8192]{2,1,0:T(2,128)(2,1)} reshape(bf16[256,8192]{1,0:T(8,128)(2,1)} %reduce.3) | data formatting | bytes 8388608
  226.9 0.0 copy-start.1
  226.9 37.9 %all-to-all-done.1 = bf16[128,2,8192]{2,1,0:T(2,128)(2,1)} async-done(((bf16[128,2,8192]{2,1,0:T(2,128)(2,1)}), bf16[128,2,8192]{2,1,0:T(2,128)(2,1)}, u32[]{:S(2)}, u32[]{:S(2)}) %all-to-all-start.1) | async-done | bytes 4194336 | tf_op jit(solution)/shard_map/all_to_all | solution.py:77
  264.8 5.8 %all-to-all-start.3 = ((bf16[128,2,8192]{2,1,0:T(2,128)(2,1)}), bf16[128,2,8192]{2,1,0:T(2,128)(2,1)}, u32[]{:S(2)}, u32[]{:S(2)}) async-start(bf16[128,2,8192]{2,1,0:T(2,128)(2,1)} %reshape.188), calls=%async_computation.3 | async-start | bytes 8388608 | tf_op jit(solution)/shard_map/all_to_all | solution.py:78
  270.6 0.0 reduce-scatter.2.cloned.1.call-start
  270.7 0.0 copy-done.1
  270.7 19.8 %reshape.187 = bf16[256,1,8192]{2,1,0:T(2,128)(2,1)} reshape(bf16[128,2,8192]{2,1,0:T(2,128)(2,1)} %all-to-all-done.1) | data formatting | bytes 8388608
  290.5 26.3 %reduce = bf16[256,8192]{1,0:T(8,128)(2,1)} reduce(bf16[256,1,8192]{2,1,0:T(2,128)(2,1)} %reshape.187, bf16[]{:T(256)} %constant.117), dimensions={1}, to_apply=%all_to_all.32.reduce_sub_computation | reduce | bytes 8388610 | tf_op jit(solution)/shard_map/all_to_all | solution.py:77
  316.8 7.7 %all_to_all.33 = bf16[128,2,1,8192]{3,1,0,2:T(2,128)(2,1)} reshape(bf16[256,8192]{1,0:T(8,128)(2,1)} %reduce) | data formatting | bytes 8388608 | tf_op jit(solution)/shard_map/all_to_all | solution.py:77
  324.5 6.9 %copy.29 = bf16[2,128,1,8192]{3,1,0,2:T(8,128)(2,1)} copy(bf16[2,128,1,8192]{3,0,1,2:T(2,128)(2,1)} %bitcast.55) | data formatting | bytes 8388608 | tf_op jit(solution)/shard_map/all_to_all | solution.py:77
  331.4 0.0 all-to-all-done.3
  331.4 19.8 %reshape.189 = bf16[256,1,8192]{2,1,0:T(2,128)(2,1)} reshape(bf16[128,2,8192]{2,1,0:T(2,128)(2,1)} %all-to-all-done.3) | data formatting | bytes 8388608
  351.2 26.3 %reduce.1 = bf16[256,8192]{1,0:T(8,128)(2,1)} reduce(bf16[256,1,8192]{2,1,0:T(2,128)(2,1)} %reshape.189, bf16[]{:T(256)} %constant.117), dimensions={1}, to_apply=%all_to_all.36.reduce_sub_computation | reduce | bytes 8388610 | tf_op jit(solution)/shard_map/all_to_all | solution.py:78
  377.4 7.9 %all_to_all.37 = bf16[128,2,1,8192]{3,1,0,2:T(2,128)(2,1)} reshape(bf16[256,8192]{1,0:T(8,128)(2,1)} %reduce.1) | data formatting | bytes 8388608 | tf_op jit(solution)/shard_map/all_to_all | solution.py:78
  385.3 6.9 %copy.32 = bf16[2,128,1,8192]{3,1,0,2:T(8,128)(2,1)} copy(bf16[2,128,1,8192]{3,0,1,2:T(2,128)(2,1)} %bitcast.56) | data formatting | bytes 8388608 | tf_op jit(solution)/shard_map/all_to_all | solution.py:78
  392.2 0.0 all-gather.2.cloned.1.call-done
  392.2 20.2 %gather_fusion.1 = bf16[512,8192]{1,0:T(8,128)(2,1)} fusion(bf16[512,8192]{1,0:T(8,128)(2,1)} %all-gather.2.cloned.1.call-done, s32[1024]{0:T(1024)S(1)} %pad_clamp_fusion), kind=kCustom, calls=%fused_computation.3 | custom fusion | bytes 16779264 | tf_op jit(solution)/shard_map/jit(_take)/gather | solution.py:106
  412.4 21.5 %fusion.17 = f32[512,8192]{1,0:T(8,128)} fusion(bf16[256,8192]{1,0:T(8,128)(2,1)} %bitcast.61, bf16[256,8192]{1,0:T(8,128)(2,1)} %bitcast.59, bf16[512,8192]{1,0:T(8,128)(2,1)} %gather_fusion.1, pred[512]{0:T(512)(128)(4,1)S(1)} %compare_and_fusion.1), kind=kOutput, calls=%fused_computation.30 | convolution fusion | flops 4307681280 | bytes 33554944 | tf_op jit(solution)/shard_map/dot_general | solution.py:52
  433.8 0.0 reduce-scatter.2.cloned.1.call-update
  433.9 92.9 %reduce-scatter.2.cloned.1.call-done = f32[512,1024]{1,0:T(8,128)} async-done(((f32[512,8192]{1,0:T(8,128)}), f32[512,1024]{1,0:T(8,128)}) %reduce-scatter.2.cloned.1.call-update) | async-done | bytes 2097168 | tf_op jit(solution)/shard_map/reduce_scatter | solution.py:109
  526.7 34.8 %all_to_all.45 = f32[16,32,1024]{2,1,0:T(8,128)S(1)} all-to-all(f32[16,32,1024]{2,1,0:T(8,128)} %bitcast.63), channel_id=1, replica_groups=mesh['gx'=8,'gy'=16] {'gy'}, dimensions={0} | all-to-all | bytes 4194304 | tf_op jit(solution)/shard_map/all_to_all | solution.py:43
  561.6 0.7 reduce_sum.9
  (17 shorter events, 0.1 us)
Async XLA Ops:
  15.7 11.8 %copy-start = (bf16[32,1024]{1,0:T(8,128)(2,1)S(1)}, bf16[32,1024]{1,0:T(8,128)(2,1)}, u32[]{:S(2)}) copy-start(bf16[32,1024]{1,0:T(8,128)(2,1)} %param.9) | copy-start | bytes 196612
  15.7 84.2 %all-to-all-start = ((bf16[128,2,1,8192]{3,1,2,0:T(2,128)(2,1)}), bf16[128,2,1,8192]{3,1,2,0:T(2,128)(2,1)}, u32[]{:S(2)}, u32[]{:S(2)}) async-start(bf16[128,2,1,8192]{3,1,2,0:T(2,128)(2,1)} %bitcast.53), calls=%async_computation | async-start | bytes 8388608 | tf_op jit(solution)/shard_map/all_to_all | solution.py:36
  27.5 364.7 %all-gather.2.cloned.1.call-start = ((), (), s32[]{:S(2)}) async-start(), calls=%async_computation.6 | async-start | bytes 8912896 | tf_op jit(solution)/shard_map/all_gather | solution.py:105
  27.5 47.5 %collective-permute-start = (bf16[32,1024]{1,0:T(8,128)(2,1)S(1)}, bf16[32,1024]{1,0:T(8,128)(2,1)S(1)}, u32[]{:S(2)}, u32[]{:S(2)}) collective-permute-start(bf16[32,1024]{1,0:T(8,128)(2,1)S(1)} %copy-done), channel_id=1, source_target_pairs={{0,16},{16,32},{32,48},{48,64},{64,80},{80,96},{96,112},{112,0},{1... | collective-permute-start | bytes 196616 | tf_op jit(solution)/shard_map/ppermute | solution.py:97
  75.0 4.9 collective-permute-start.1
  75.0 4.9 collective-permute-start.4
  79.9 4.9 collective-permute-start.2
  80.0 4.9 collective-permute-start.5
  84.8 4.9 collective-permute-start.3
  84.9 5.0 collective-permute-start.6
  99.9 10.9 %copy-start.2 = (s32[256]{0:T(256)S(1)}, s32[256]{0:T(256)}, u32[]{:S(2)}) copy-start(s32[256]{0:T(256)} %param.14) | copy-start | bytes 3076
  99.9 10.9 %copy-start.3 = (s32[256]{0:T(256)S(1)}, s32[256]{0:T(256)}, u32[]{:S(2)}) copy-start(s32[256]{0:T(256)} %param.13) | copy-start | bytes 3076
  99.9 64.4 %all-to-all-start.2 = ((bf16[128,2,1,8192]{3,1,2,0:T(2,128)(2,1)}), bf16[128,2,1,8192]{3,1,2,0:T(2,128)(2,1)}, u32[]{:S(2)}, u32[]{:S(2)}) async-start(bf16[128,2,1,8192]{3,1,2,0:T(2,128)(2,1)} %bitcast.54), calls=%async_computation.2 | async-start | bytes 8388608 | tf_op jit(solution)/shard_map/all_to_all | solution.py:36
  204.8 60.0 %all-to-all-start.1 = ((bf16[128,2,8192]{2,1,0:T(2,128)(2,1)}), bf16[128,2,8192]{2,1,0:T(2,128)(2,1)}, u32[]{:S(2)}, u32[]{:S(2)}) async-start(bf16[128,2,8192]{2,1,0:T(2,128)(2,1)} %reshape.186), calls=%async_computation.1 | async-start | bytes 8388608 | tf_op jit(solution)/shard_map/all_to_all | solution.py:77
  226.9 43.8 %copy-start.1 = (s32[512]{0:T(512)S(1)}, s32[512]{0:T(512)}, u32[]{:S(2)}) copy-start(s32[512]{0:T(512)} %param.15) | copy-start | bytes 6148
  264.8 66.6 %all-to-all-start.3 = ((bf16[128,2,8192]{2,1,0:T(2,128)(2,1)}), bf16[128,2,8192]{2,1,0:T(2,128)(2,1)}, u32[]{:S(2)}, u32[]{:S(2)}) async-start(bf16[128,2,8192]{2,1,0:T(2,128)(2,1)} %reshape.188), calls=%async_computation.3 | async-start | bytes 8388608 | tf_op jit(solution)/shard_map/all_to_all | solution.py:78
  270.6 256.1 %reduce-scatter.2.cloned.1.call-start = ((), (), s32[]{:S(2)}) async-start(), calls=%async_computation.7 | async-start | bytes 18874368 | tf_op jit(solution)/shard_map/reduce_scatter | solution.py:109
Sparse Core Ops, SparseCore 0:
  91.4 116.0 all-gather.1
  434.0 92.7 reduce-scatter.1
